TPU v7x, 32 devices: a whole 2x2x4 slice. The times are simulated.
32 devices in a mesh: grp: 8 (over y, x, core), tile: 4 (over z).
Axes of the slice: x: 2, y: 2, z: 4, core: 2. Of those that a mesh axis runs over, the one named last changes fastest.
Arguments:
- atm_flux: float32 [6, 32768], P(None, ('grp', 'tile')), may hold values from -6 to 6
- send_block: int32 [32, 4, 4], P(('grp', 'tile')), may hold values from 0 to 7
- send_count: int32 [32, 4], P(('grp', 'tile')), may hold values from 1 to 4, as said below
- recv_block: int32 [32, 4, 4], P(('grp', 'tile')), may hold values from 0 to 63
- recv_weight: bfloat16 [32, 4, 4, 128, 128], P(('grp', 'tile')), may hold values from -0.5 to 0.5
- sea_temp: float32 [256, 1024], P('grp', 'tile'), may hold values from -6 to 6
- ocean_mask: int32 [256, 1024], P('grp', 'tile'), may hold values 0 or 1
Outputs:
- heat_flux: float32 [256, 1024], P('grp', 'tile')
- stress_curl: float32 [256, 1024], P('grp', 'tile')
- atm_return: float32 [4, 32768], P(None, ('grp', 'tile'))
Inputs may be any that keep to these rules, and one draw needn't show every extreme that they name: `send_count`: in every draw a quarter of the tile indices, drawn from the seed, receive exactly 4 blocks from every device of their group; every other pair carries 1 to 2 blocks.
All inputs are finite; a program needn't handle non-finite values. No bound on the sum of `ocean_mask` on one device may be relied on, other than what follows from the above.
Results may differ from a plain program's by a relative error of at most 0.0003.
Values sent between devices are 32-bit elements; how exact they have to be, the bound alone decides.
A program may use at most 64 MiB of HBM per device.

v0:
```python
import jax
import jax.numpy as jnp
from jax import lax
from jax.sharding import PartitionSpec as P

precise = lax.Precision.HIGHEST


def extended(block, sides, width):
    for axis, dim in sides:
        count = lax.axis_size(axis)
        forward = [(i, i + 1) for i in range(count - 1)]
        forward.append((count - 1, 0))
        backward = [(target, source) for source, target in forward]
        low = lax.ppermute(
            lax.slice_in_dim(block, block.shape[dim] - width, None, axis=dim), axis, forward
        )
        high = lax.ppermute(lax.slice_in_dim(block, 0, width, axis=dim), axis, backward)
        block = jnp.concatenate([low, block, high], axis=dim)
    return block


def from_partner(value, axis, stride):
    return lax.ppermute(value, axis, [(i, i ^ 1 << stride) for i in range(lax.axis_size(axis))])


def bulk_formula(fields, surface_temp, ocean_mask):
    sea_share = ocean_mask.astype(jnp.float32)
    wind_u, wind_v, air_temp, air_vapor, short_down, long_down = [fields[k] for k in range(6)]
    wind_speed = jnp.sqrt(wind_u * wind_u + wind_v * wind_v + 0.5)
    stress_x = 0.8 * wind_speed * wind_u * sea_share
    stress_y = 0.8 * wind_speed * wind_v * sea_share
    sensible = 0.6 * wind_speed * (surface_temp - air_temp)
    latent = 0.7 * wind_speed * (jnp.exp(0.3 * surface_temp) - air_vapor)
    long_up = 0.4 * (1.0 + 0.2 * surface_temp) ** 4
    heat_flux = (0.94 * short_down + long_down - long_up - sensible - latent) * sea_share
    surface = jnp.stack([surface_temp, sensible, latent, long_up]) * sea_share[None]
    return (stress_x, stress_y, heat_flux, surface)


def per_device(atm_flux, send_block, send_count, recv_block, recv_weight, sea_temp, ocean_mask):
    tile_count = lax.axis_size("tile")
    field_count = atm_flux.shape[0]
    block_cells = recv_weight.shape[-1]
    slot_count = send_block.shape[2]
    atm_blocks = atm_flux.shape[1] // block_cells
    ocean_rows, ocean_cols = sea_temp.shape
    ocean_blocks = ocean_rows * ocean_cols // block_cells
    slot_range = jnp.arange(slot_count, dtype=jnp.int32)
    blocks = atm_flux.reshape(field_count, atm_blocks, block_cells)
    send_index = send_block[0]
    pair_count = send_count[0]
    live_slots = (slot_range[None, :] < pair_count[:, None]).astype(jnp.float32)
    chosen = jnp.take(blocks, send_index, axis=1) * live_slots[None, :, :, None]
    incoming = lax.all_to_all(chosen, "tile", split_axis=1, concat_axis=1, tiled=True)
    weight_wide = recv_weight[0].astype(jnp.float32)
    remapped = jnp.einsum("scij,fscj->fsci", weight_wide, incoming, precision=precise)
    dest_block = recv_block[0]
    onehot = (
        jnp.arange(ocean_blocks, dtype=jnp.int32)[:, None] == dest_block.reshape(-1)[None, :]
    ).astype(jnp.float32)
    landed = jnp.einsum(
        "ok,fkj->foj",
        onehot,
        remapped.reshape(field_count, tile_count * slot_count, block_cells),
        precision=precise,
    )
    fields = landed.reshape(field_count, ocean_rows, ocean_cols)
    stress_x, stress_y, heat_flux, surface = bulk_formula(fields, sea_temp, ocean_mask)
    sea_share = ocean_mask.astype(jnp.float32)
    padded = extended(jnp.stack([stress_x, stress_y]), (("grp", 1), ("tile", 2)), 1)
    mirror_row = stress_x[ocean_rows - 1]
    for bit_number in range(tile_count.bit_length() - 1):
        mirror_row = from_partner(mirror_row, "tile", bit_number)
    fold_values = -jnp.flip(mirror_row)
    group_index = lax.axis_index("grp")
    south_rim = jnp.where(group_index == 0, 0.0, padded[0, 0, 1:-1])
    north_rim = jnp.where(group_index == lax.axis_size("grp") - 1, fold_values, padded[0, -1, 1:-1])
    column_x = jnp.concatenate([south_rim[None], stress_x, north_rim[None]], axis=0)
    stress_curl = 0.5 * (padded[1, 1:-1, 2:] - padded[1, 1:-1, :-2]) - 0.5 * (
        column_x[2:] - column_x[:-2]
    )
    stress_curl = stress_curl * sea_share
    surface_blocks = surface.reshape(surface.shape[0], ocean_blocks, block_cells)
    chosen_back = jnp.take(surface_blocks, dest_block, axis=1)
    returned = jnp.einsum("scij,fsci->fscj", weight_wide, chosen_back, precision=precise)
    arrived = lax.all_to_all(returned, "tile", split_axis=1, concat_axis=1, tiled=True)
    arrived = arrived * live_slots[None, :, :, None]
    atm_onehot = (
        jnp.arange(atm_blocks, dtype=jnp.int32)[:, None] == send_index.reshape(-1)[None, :]
    ).astype(jnp.float32)
    atm_part = jnp.einsum(
        "ak,fkj->faj",
        atm_onehot,
        arrived.reshape(surface.shape[0], tile_count * slot_count, block_cells),
        precision=precise,
    )
    return (heat_flux, stress_curl, atm_part.reshape(surface.shape[0], atm_blocks * block_cells))


def solution(mesh):
    placed = (
        P(None, ("grp", "tile")),
        P(("grp", "tile"), None, None),
        P(("grp", "tile"), None),
        P(("grp", "tile"), None, None),
        P(("grp", "tile"), None, None, None, None),
        P("grp", "tile"),
        P("grp", "tile"),
    )
    return jax.shard_map(
        per_device,
        mesh=mesh,
        in_specs=placed,
        out_specs=(P("grp", "tile"), P("grp", "tile"), P(None, ("grp", "tile"))),
        check_vma=False,
    )
```

profile of v0, /device:TPU:0, one launch (start us, length us, event | category | flops | bytes accessed | tf_op | source)
XLA Modules:
  0.0 37.9 jit_solution(13872398486308174749)
XLA Ops:
  0.6 0.0 copy-start
  0.6 0.7 %compare_select_fusion.2 = s32[4,4,1]{1,0,2:T(4,128)S(1)} fusion(s32[1,4,4]{2,1,0:T(4,128)} %param.8), kind=kLoop, calls=%fused_computation.52 | loop fusion | flops 48 | bytes 128 | tf_op jit(solution)/shard_map/jit(_take)/jit(_where)/select_n | solution.py:54
  1.4 0.1 reshape.162
  1.5 0.0 copy-start.4
  1.5 0.0 copy-start.7
  1.5 0.7 %copy-done.4 = s32[1,4,4]{2,1,0:T(4,128)S(1)} copy-done((s32[1,4,4]{2,1,0:T(4,128)S(1)}, s32[1,4,4]{2,1,0:T(4,128)}, u32[]{:S(2)}) %copy-start.4) | copy-done | bytes 88
  2.2 0.0 copy-done.7
  2.2 0.1 fusion.25
  2.2 1.3 %gather_fusion = f32[16,6,128]{2,1,0:T(8,128)S(1)} fusion(f32[6,8,128]{2,0,1:T(8,128)} %bitcast.69, s32[1024]{0:T(1024)S(1)} %pad_clamp_fusion.1), kind=kCustom, calls=%fused_computation | custom fusion | bytes 98368 | tf_op jit(solution)/shard_map/jit(_take)/gather | solution.py:54
  3.6 0.7 %fusion.6 = f32[6,4,4,128]{3,2,0,1:T(4,128)} fusion(f32[4,4,6,128]{3,2,1,0:T(8,128)S(1)} %bitcast.65, f32[4,4]{1,0:T(4,128)S(1)} %get-tuple-element.21, pred[4,4]{1,0:T(4,128)(4,1)S(1)} %get-tuple-element.22), kind=kLoop, calls=%fused_computation.14 | loop fusion | flops 24576 | bytes 98384 | tf_op jit(solution)/shard_map/mul | solution.py:54
  4.3 0.0 copy-start.3
  4.3 0.0 copy-start.2
  4.3 6.5 %all-to-all-start = ((f32[6,4,4,128]{3,2,0,1:T(4,128)}), f32[6,4,4,128]{3,2,0,1:T(4,128)S(1)}, u32[]{:S(2)}, u32[]{:S(2)}) async-start(f32[6,4,4,128]{3,2,0,1:T(4,128)} %fusion.6), calls=%async_computation | async-start | bytes 98304 | tf_op jit(solution)/shard_map/all_to_all | solution.py:55
  10.7 0.0 copy-done.3
  10.7 0.1 eq.37
  10.8 0.1 eq.43
  10.9 0.0 copy-done.2
  10.9 0.0 copy-start.1
  11.0 0.7 %copy-done.1 = s32[32,256]{1,0:T(8,128)S(1)} copy-done((s32[32,256]{1,0:T(8,128)S(1)}, s32[32,256]{1,0:T(8,128)}, u32[]{:S(2)}) %copy-start.1) | copy-done | bytes 32792
  11.7 0.1 reshape.170
  11.8 4.7 %all-to-all-done = f32[6,4,4,128]{3,2,0,1:T(4,128)S(1)} async-done(((f32[6,4,4,128]{3,2,0,1:T(4,128)}), f32[6,4,4,128]{3,2,0,1:T(4,128)S(1)}, u32[]{:S(2)}, u32[]{:S(2)}) %all-to-all-start) | async-done | bytes 49184 | tf_op jit(solution)/shard_map/all_to_all | solution.py:55
  16.4 0.0 copy-done
  16.4 0.9 %fusion.1 = f32[4,4,6,128]{3,2,1,0:T(8,128)S(1)} fusion(bf16[1,4,4,128,128]{4,3,2,1,0:T(8,128)(2,1)S(1)} %copy-done, f32[6,4,4,128]{3,2,0,1:T(4,128)S(1)} %all-to-all-done), kind=kOutput, calls=%fused_computation.6 | convolution fusion | flops 18874368 | bytes 622592 | tf_op jit(solution)/shard_map/scij,fscj->fsci/dot_general | solution.py:57
  17.4 0.4 convolution_bitcast_fusion
  17.8 0.7 %multiply_bitcast_fusion = (f32[1,32,256]{2,1,0:T(8,128)S(1)}, f32[32,256]{1,0:T(8,128)S(1)}, f32[32,256]{1,0:T(8,128)}, f32[32,256]{1,0:T(8,128)S(1)}, f32[32,256]{1,0:T(8,128)S(1)}, /*index=5*/f32[32,256]{1,0:T(8,128)S(1)}) fusion(f32[32,256]{1,0:T(8,128)S(1)} %squeeze.40, s32[32,256]{1,0:T(8,128)S(1)} %copy-done.1, f32[32,256]{1,0:T(8,128)S(1)} %squeeze.39, ...), kind=kLoop, calls=%fused_computation.37 | loop fusion | flops 212992 | bytes 425984 | tf_op jit(solution)/shard_map/stack | solution.py:71
  18.5 0.1 collective-permute-start
  18.6 2.6 %collective-permute-start.1 = (f32[2,1,256]{2,1,0:T(1,128)S(1)}, f32[2,1,256]{2,1,0:T(1,128)S(1)}, u32[]{:S(2)}, u32[]{:S(2)}) collective-permute-start(f32[2,1,256]{2,1,0:T(1,128)S(1)} %get-tuple-element.18), channel_id=1, source_target_pairs={{4,0},{8,4},{12,8},{16,12},{20,16},{24,20},{28,24},{0,28},{5,1},{9... | collective-permute-start | bytes 6152 | tf_op jit(solution)/shard_map/ppermute | solution.py:18
  21.2 0.8 %collective-permute-start.4 = (f32[256]{0:T(256)S(1)}, f32[256]{0:T(256)S(1)}, u32[]{:S(2)}, u32[]{:S(2)}) collective-permute-start(f32[256]{0:T(256)S(1)} %bitcast.73), channel_id=1, source_target_pairs={{0,1},{1,0},{2,3},{3,2},{4,5},{5,4},{6,7},{7,6},{8,9},{9,8},{10,11... | collective-permute-start | bytes 3080 | tf_op jit(solution)/shard_map/ppermute | solution.py:24
  22.2 0.1 maximum_multiply_fusion
  22.3 0.6 %gather_fusion.1 = f32[16,4,128]{2,1,0:T(4,128)S(1)} fusion(f32[4,64,128]{2,0,1:T(4,128)S(1)} %maximum_multiply_fusion, s32[1024]{0:T(1024)S(1)} %pad_clamp_fusion), kind=kCustom, calls=%fused_computation.1 | custom fusion | bytes 65600 | tf_op jit(solution)/shard_map/jit(_take)/gather | solution.py:85
  22.9 1.2 %convolution_bitcast_fusion.1 = f32[4,4,4,128]{3,0,2,1:T(4,128)} fusion(bf16[1,4,4,128,128]{4,3,2,1,0:T(8,128)(2,1)S(1)} %copy-done, f32[4,4,4,128]{3,2,1,0:T(4,128)S(1)} %bitcast.68, pred[4,4]{1,0:T(4,128)(4,1)S(1)} %compare_and_fusion), kind=kOutput, calls=%fused_computation.3 | convolution fusion | flops 12591104 | bytes 589840 | tf_op jit(solution)/shard_map/scij,fsci->fscj/dot_general | solution.py:86
  24.1 3.3 %all-to-all-start.1 = ((f32[4,4,4,128]{3,0,2,1:T(4,128)}), f32[4,4,4,128]{3,0,2,1:T(4,128)S(1)}, u32[]{:S(2)}, u32[]{:S(2)}) async-start(f32[4,4,4,128]{3,0,2,1:T(4,128)} %convolution_bitcast_fusion.1), calls=%async_computation.1 | async-start | bytes 65536 | tf_op jit(solution)/shard_map/all_to_all | solution.py:87
  27.4 0.0 collective-permute-done.4
  27.4 2.9 %collective-permute-start.5 = (f32[256]{0:T(256)S(1)}, f32[256]{0:T(256)S(1)}, u32[]{:S(2)}, u32[]{:S(2)}) collective-permute-start(f32[256]{0:T(256)S(1)} %collective-permute-done.4), channel_id=1, source_target_pairs={{0,2},{1,3},{2,0},{3,1},{4,6},{5,7},{6,4},{7,5},{8,10},{9,11},{10,... | collective-permute-start | bytes 3080 | tf_op jit(solution)/shard_map/ppermute | solution.py:24
  30.3 0.0 collective-permute-done
  30.3 0.0 collective-permute-done.1
  30.3 0.0 copy-start.5
  30.3 0.1 fusion.29
  30.4 1.5 %collective-permute-start.3 = (f32[2,34,1]{2,1,0:T(8,128)S(1)}, f32[2,34,1]{2,1,0:T(8,128)S(1)}, u32[]{:S(2)}, u32[]{:S(2)}) collective-permute-start(f32[2,34,1]{2,1,0:T(8,128)S(1)} %get-tuple-element.17), channel_id=1, source_target_pairs={{0,1},{1,2},{2,3},{3,0},{4,5},{5,6},{6,7},{7,4},{8,9},{9,10},{10,1... | collective-permute-start | bytes 824 | tf_op jit(solution)/shard_map/ppermute | solution.py:15
  31.9 2.4 %collective-permute-start.2 = (f32[2,34,1]{2,1,0:T(8,128)S(1)}, f32[2,34,1]{2,1,0:T(8,128)S(1)}, u32[]{:S(2)}, u32[]{:S(2)}) collective-permute-start(f32[2,34,1]{2,1,0:T(8,128)S(1)} %get-tuple-element.16), channel_id=1, source_target_pairs={{1,0},{2,1},{3,2},{0,3},{5,4},{6,5},{7,6},{4,7},{9,8},{10,9},{11,1... | collective-permute-start | bytes 824 | tf_op jit(solution)/shard_map/ppermute | solution.py:18
  34.2 0.0 copy-done.5
  34.2 0.0 collective-permute-done.5
  34.2 0.1 rev.4
  34.3 0.0 slice-start
  34.3 0.7 %slice-done = f32[1,1,256]{2,1,0:T(1,128)S(1)} async-done(((f32[2,1,256]{2,1,0:T(1,128)}), f32[1,1,256]{2,1,0:T(1,128)S(1)}, s32[]{:S(2)}) %slice-start) | async-done | bytes 1048 | tf_op jit(solution)/shard_map/slice | solution.py:78
  35.0 0.0 copy-start.6
  35.0 1.3 %collective-permute-done.3 = f32[2,34,1]{2,1,0:T(8,128)S(1)} collective-permute-done((f32[2,34,1]{2,1,0:T(8,128)S(1)}, f32[2,34,1]{2,1,0:T(8,128)S(1)}, u32[]{:S(2)}, u32[]{:S(2)}) %collective-permute-start.3) | collective-permute-done | bytes 304 | tf_op jit(solution)/shard_map/ppermute | solution.py:15
  36.3 0.0 collective-permute-done.2
  36.3 0.0 copy-done.6
  36.3 0.7 %fusion.10 = f32[32,256]{1,0:T(8,128)} fusion(f32[32,256]{1,0:T(8,128)S(1)} %get-tuple-element.12, f32[1,256]{1,0:T(1,128)S(1)} %fusion.26, f32[1,256]{1,0:T(1,128)S(1)} %bitcast.72, f32[2,34,1]{2,1,0:T(8,128)S(1)} %collective-permute-done.3, f32[2,1,256]{2,1,0:T(1,128)S(1)} %copy-done.6, f32[2,1,256]{2,1,0:T(1,128)S(1)} %collective-permute-done, ...), kind=kLoop, calls=%fused_computation.19 | loop fusion | flops 139264 | bytes 170528 | tf_op jit(solution)/shard_map/mul | solution.py:83
  37.0 0.0 all-to-all-done.1
  37.0 0.1 broadcast_multiply_fusion
  37.1 0.1 convolution_bitcast_fusion.2
  37.2 0.6 %copy.32 = f32[1,4,8,128]{3,1,2,0:T(4,128)} copy(f32[1,4,8,128]{3,2,1,0:T(8,128)S(1)} %convolution_bitcast_fusion.2) | data formatting | bytes 32768
  (21 shorter events, 0.3 us)
Async XLA Ops:
  0.6 15.8 %copy-start = (bf16[1,4,4,128,128]{4,3,2,1,0:T(8,128)(2,1)S(1)}, bf16[1,4,4,128,128]{4,3,2,1,0:T(8,128)(2,1)}, u32[]{:S(2)}) copy-start(bf16[1,4,4,128,128]{4,3,2,1,0:T(8,128)(2,1)} %param.11) | copy-start | bytes 1572868
  1.5 0.7 %copy-start.4 = (s32[1,4,4]{2,1,0:T(4,128)S(1)}, s32[1,4,4]{2,1,0:T(4,128)}, u32[]{:S(2)}) copy-start(s32[1,4,4]{2,1,0:T(4,128)} %param.8) | copy-start | bytes 196
  1.5 0.7 %copy-start.7 = (s32[1,4]{1,0:T(1,128)S(1)}, s32[1,4]{1,0:T(1,128)}, u32[]{:S(2)}) copy-start(s32[1,4]{1,0:T(1,128)} %param.9) | copy-start | bytes 52
  4.3 6.5 %copy-start.3 = (s32[1,4,4]{2,1,0:T(4,128)S(1)}, s32[1,4,4]{2,1,0:T(4,128)}, u32[]{:S(2)}) copy-start(s32[1,4,4]{2,1,0:T(4,128)} %param.10) | copy-start | bytes 196
  4.3 6.7 %copy-start.2 = (f32[32,256]{1,0:T(8,128)S(1)}, f32[32,256]{1,0:T(8,128)}, u32[]{:S(2)}) copy-start(f32[32,256]{1,0:T(8,128)} %param.12) | copy-start | bytes 98308
  4.3 12.2 %all-to-all-start = ((f32[6,4,4,128]{3,2,0,1:T(4,128)}), f32[6,4,4,128]{3,2,0,1:T(4,128)S(1)}, u32[]{:S(2)}, u32[]{:S(2)}) async-start(f32[6,4,4,128]{3,2,0,1:T(4,128)} %fusion.6), calls=%async_computation | async-start | bytes 98304 | tf_op jit(solution)/shard_map/all_to_all | solution.py:55
  10.9 0.8 %copy-start.1 = (s32[32,256]{1,0:T(8,128)S(1)}, s32[32,256]{1,0:T(8,128)}, u32[]{:S(2)}) copy-start(s32[32,256]{1,0:T(8,128)} %param.13) | copy-start | bytes 98308
  18.5 11.7 %collective-permute-start = (f32[2,1,256]{2,1,0:T(1,128)S(1)}, f32[2,1,256]{2,1,0:T(1,128)S(1)}, u32[]{:S(2)}, u32[]{:S(2)}) collective-permute-start(f32[2,1,256]{2,1,0:T(1,128)S(1)} %get-tuple-element.19), channel_id=1, source_target_pairs={{0,4},{4,8},{8,12},{12,16},{16,20},{20,24},{24,28},{28,0},{1,5},{5... | collective-permute-start | bytes 6152 | tf_op jit(solution)/shard_map/ppermute | solution.py:15
  18.6 11.7 %collective-permute-start.1 = (f32[2,1,256]{2,1,0:T(1,128)S(1)}, f32[2,1,256]{2,1,0:T(1,128)S(1)}, u32[]{:S(2)}, u32[]{:S(2)}) collective-permute-start(f32[2,1,256]{2,1,0:T(1,128)S(1)} %get-tuple-element.18), channel_id=1, source_target_pairs={{4,0},{8,4},{12,8},{16,12},{20,16},{24,20},{28,24},{0,28},{5,1},{9... | collective-permute-start | bytes 6152 | tf_op jit(solution)/shard_map/ppermute | solution.py:18
  21.2 6.2 %collective-permute-start.4 = (f32[256]{0:T(256)S(1)}, f32[256]{0:T(256)S(1)}, u32[]{:S(2)}, u32[]{:S(2)}) collective-permute-start(f32[256]{0:T(256)S(1)} %bitcast.73), channel_id=1, source_target_pairs={{0,1},{1,0},{2,3},{3,2},{4,5},{5,4},{6,7},{7,6},{8,9},{9,8},{10,11... | collective-permute-start | bytes 3080 | tf_op jit(solution)/shard_map/ppermute | solution.py:24
  24.1 12.9 %all-to-all-start.1 = ((f32[4,4,4,128]{3,0,2,1:T(4,128)}), f32[4,4,4,128]{3,0,2,1:T(4,128)S(1)}, u32[]{:S(2)}, u32[]{:S(2)}) async-start(f32[4,4,4,128]{3,0,2,1:T(4,128)} %convolution_bitcast_fusion.1), calls=%async_computation.1 | async-start | bytes 65536 | tf_op jit(solution)/shard_map/all_to_all | solution.py:87
  27.4 6.8 %collective-permute-start.5 = (f32[256]{0:T(256)S(1)}, f32[256]{0:T(256)S(1)}, u32[]{:S(2)}, u32[]{:S(2)}) collective-permute-start(f32[256]{0:T(256)S(1)} %collective-permute-done.4), channel_id=1, source_target_pairs={{0,2},{1,3},{2,0},{3,1},{4,6},{5,7},{6,4},{7,5},{8,10},{9,11},{10,... | collective-permute-start | bytes 3080 | tf_op jit(solution)/shard_map/ppermute | solution.py:24
  30.3 3.9 %copy-start.5 = (f32[2,1,256]{2,1,0:T(1,128)}, f32[2,1,256]{2,1,0:T(1,128)S(1)}, u32[]{:S(2)}) copy-start(f32[2,1,256]{2,1,0:T(1,128)S(1)} %collective-permute-done.1) | copy-start | bytes 6148
  30.4 5.9 %collective-permute-start.3 = (f32[2,34,1]{2,1,0:T(8,128)S(1)}, f32[2,34,1]{2,1,0:T(8,128)S(1)}, u32[]{:S(2)}, u32[]{:S(2)}) collective-permute-start(f32[2,34,1]{2,1,0:T(8,128)S(1)} %get-tuple-element.17), channel_id=1, source_target_pairs={{0,1},{1,2},{2,3},{3,0},{4,5},{5,6},{6,7},{7,4},{8,9},{9,10},{10,1... | collective-permute-start | bytes 824 | tf_op jit(solution)/shard_map/ppermute | solution.py:15
  31.9 4.4 %collective-permute-start.2 = (f32[2,34,1]{2,1,0:T(8,128)S(1)}, f32[2,34,1]{2,1,0:T(8,128)S(1)}, u32[]{:S(2)}, u32[]{:S(2)}) collective-permute-start(f32[2,34,1]{2,1,0:T(8,128)S(1)} %get-tuple-element.16), channel_id=1, source_target_pairs={{1,0},{2,1},{3,2},{0,3},{5,4},{6,5},{7,6},{4,7},{9,8},{10,9},{11,1... | collective-permute-start | bytes 824 | tf_op jit(solution)/shard_map/ppermute | solution.py:18
  34.3 0.7 %slice-start = ((f32[2,1,256]{2,1,0:T(1,128)}), f32[1,1,256]{2,1,0:T(1,128)S(1)}, s32[]{:S(2)}) async-start(f32[2,1,256]{2,1,0:T(1,128)} %copy-done.5), calls=%async_computation.2 | async-start | bytes 2048 | tf_op jit(solution)/shard_map/slice | solution.py:78
  35.0 1.3 %copy-start.6 = (f32[2,1,256]{2,1,0:T(1,128)S(1)}, f32[2,1,256]{2,1,0:T(1,128)}, u32[]{:S(2)}) copy-start(f32[2,1,256]{2,1,0:T(1,128)} %copy-done.5) | copy-start | bytes 6148
where the time goes:
time: 38.4 us; the launch traced here: 37.9 us
  starting transfers between devices  20 us (52%)
  waiting for transfers between devices  5.95 us (15%)
  local copies, waits for them, and re-layouts  5.32 us (14%)
  other arithmetic  3.19 us (8%)
  matrix products  2.61 us (7%)
  between operations  0.82 us (2%)
    all_to_all x1, starting transfers between devices, per_device(): lax.all_to_all(chosen, 'tile', split_axis=1, concat_axis=1, tiled=True)  6.48 us
    ppermute x2, starting transfers between devices, extended(): lax.ppermute(lax.slice_in_dim(block, 0, width, axis=dim), axis, backward)  4.99 us
    all_to_all x1, waiting for transfers between devices, per_device(): lax.all_to_all(chosen, 'tile', split_axis=1, concat_axis=1, tiled=True)  4.65 us
    ppermute x2, starting transfers between devices, from_partner(): lax.ppermute(value, axis, [(i, i ^ 1 << stride) for i in range(lax.axis_s...  3.71 us
    all_to_all x1, starting transfers between devices, per_device(): lax.all_to_all(returned, 'tile', split_axis=1, concat_axis=1, tiled=True)  3.26 us
    unnamed x17, local copies, waits for them, and re-layouts  2.03 us
    ppermute x2, starting transfers between devices, extended(): lax.ppermute(lax.slice_in_dim(block, block.shape[dim] - width, None, axis...  1.53 us
    gather x1, local copies, waits for them, and re-layouts, per_device(): chosen = jnp.take(blocks, send_index, axis=1) * live_slots[None, :, :, None]  1.31 us
  transfers between devices with their start and end apart: 8, of which 2 were waited for; matrix products, arithmetic and copies ran while one was open for 9% of the time, Pallas kernels for 0%

commit v1 on v0

v1 whole, which is shorter than its diff:
```python
import functools

import jax
import jax.numpy as jnp
from jax import lax
from jax.experimental import pallas as pl
from jax.experimental.pallas import tpu as pltpu
from jax.sharding import PartitionSpec as P

MESH = pl.DeviceIdType.MESH
f32, bf16 = jnp.float32, jnp.bfloat16


def split(x):
    hi = x.astype(bf16).astype(f32)
    return hi, x - hi


def iota(shape, dim):
    return lax.broadcasted_iota(jnp.int32, shape, dim)


def kernel(dims, atm, sblk, scnt, rblk, wgt, temp, mask, heat, curl, ret_out,
           atm_v, sblk_s, scnt_s, rblk_s, w_v, temp_v, mask_v, send_v, recv_v, rhs_v, surf_v,
           back_v, ret_v, rim_s, rim_r, heat_v, curl_v, out_v,
           in_sem, send_sem, recv_sem, bsend_sem, brecv_sem, hsend_sem, hrecv_sem, out_sem):
    G, T, NF, NB, C, B, A, R, H = dims
    nk = T * C
    g = lax.axis_index("grp")
    t = lax.axis_index("tile")
    pow2 = T & (T - 1) == 0
    target = (lambda d: t ^ d) if pow2 else (lambda d: lax.rem(t + d, T))
    source = (lambda d: t ^ d) if pow2 else (lambda d: lax.rem(t + T - d, T))

    bar = pltpu.get_barrier_semaphore()
    for d in range(1, T):
        pl.semaphore_signal(bar, inc=1, device_id=(g, target(d)), device_id_type=MESH)

    @pl.when(g > 0)
    def _():
        pl.semaphore_signal(bar, inc=1, device_id=(g - 1, t), device_id_type=MESH)

    @pl.when(g < G - 1)
    def _():
        pl.semaphore_signal(bar, inc=1, device_id=(g + 1, t), device_id_type=MESH)

    loads = [
        pltpu.make_async_copy(src, dst, in_sem.at[k])
        for k, (src, dst) in enumerate(
            [(sblk, sblk_s), (scnt, scnt_s), (atm, atm_v), (rblk, rblk_s), (temp, temp_v), (mask, mask_v), (wgt, w_v)]
        )
    ]
    for load in loads:
        load.start()
    for load in loads[:3]:
        load.wait()

    flux = [atm_v[:, b * B : (b + 1) * B] for b in range(A)]
    wanted = {}
    for d in range(T):
        u = target(d)
        count = scnt_s[0, u]
        for c in range(C):
            live = jnp.clip(count - c, 0, 1)
            wanted[d, c] = (sblk_s[0, u, c] + 1) * live - 1
            home = jnp.full((NF, B), wanted[d, c], jnp.int32)
            block = jnp.zeros((NF, B), f32)
            for b in range(A):
                block = jnp.where(home == b, flux[b], block)
            for f in range(NF):
                send_v[d, f * C + c : f * C + c + 1, :] = block[f : f + 1]

    pl.semaphore_wait(bar, T - 1 + (g > 0).astype(jnp.int32) + (g < G - 1).astype(jnp.int32))
    outgoing = {}
    for d in range(T - 1, 0, -1):
        outgoing[d] = pltpu.make_async_remote_copy(
            send_v.at[d], recv_v.at[d], send_sem.at[d], recv_sem.at[d],
            device_id=(g, target(d)), device_id_type=MESH)
        outgoing[d].start()

    for load in loads[3:6]:
        load.wait()
    halves = lambda ref: jnp.concatenate([ref[:, h * B : (h + 1) * B] for h in range(H)], axis=0)
    sea = halves(temp_v)
    share = halves(mask_v).astype(f32)
    vapor = jnp.exp(0.3 * sea)
    base = 1.0 + 0.2 * sea
    base = base * base
    long_up = 0.4 * (base * base)
    lane = iota((8, 2 * nk), 1)
    place = jnp.full((8, 2 * nk), -1, jnp.int32)
    spots = {}
    for d in range(T):
        for c in range(C):
            o = rblk_s[0, source(d), c]
            spots[d, c] = o
            k = d * C + c
            place = jnp.where((lane == k) | (lane == nk + k), o, place)
    where_row = iota((H * R, 2 * nk), 0)
    where_row = (where_row % R) * H + where_row // R
    onehot = (where_row == place[0:1]).astype(f32).astype(bf16)
    row8 = iota((8, B), 0)
    homes = []
    for d in range(T):
        for c in range(0, C, 2):
            homes.append(jnp.where(row8 < NB, wanted[d, c], wanted[d, c + 1]))
    loads[6].wait()

    rowf = iota((NF * C, B), 0) % C
    for d in range(T):
        if d:
            outgoing[d].wait_recv()
        held = send_v[0] if d == 0 else recv_v[d]
        hi, lo = split(held)
        lhs = jnp.concatenate([hi, lo], axis=0).astype(bf16)
        weight = w_v[0, source(d)].reshape(C * B, B)
        prod = lax.dot_general(lhs, weight, (((1,), (1,)), ((), ())), preferred_element_type=f32)
        prod = prod[: NF * C] + prod[NF * C :]
        mine = prod[:, :B]
        for c in range(1, C):
            mine = jnp.where(rowf == c, prod[:, c * B : (c + 1) * B], mine)
        for f in range(NF):
            rhs_v[d * C : (d + 1) * C, f * B : (f + 1) * B] = mine[f * C : (f + 1) * C]

    hi, lo = split(rhs_v[...])
    landed = jnp.dot(onehot, jnp.concatenate([hi, lo], axis=0).astype(bf16), preferred_element_type=f32)
    wind_u, wind_v, air_temp, air_vapor, short_down, long_down = [landed[:, f * B : (f + 1) * B] for f in range(NF)]
    speed = jnp.sqrt(wind_u * wind_u + wind_v * wind_v + 0.5)
    stress_x = 0.8 * speed * wind_u * share
    stress_y = 0.8 * speed * wind_v * share

    for h in range(H):
        rim_s[0, h : h + 1, :] = stress_x[(h + 1) * R - 1 : (h + 1) * R]
        rim_s[1, h : h + 1, :] = stress_x[h * R : h * R + 1]
    diag = iota((R, B), 0) == iota((R, B), 1)
    west_edge = stress_y[:R, 0:1]
    east_edge = stress_y[(H - 1) * R :, B - 1 : B]
    rim_s[2, 0:1, :] = jnp.sum(jnp.where(diag, east_edge, 0.0), axis=0, keepdims=True)
    rim_s[3, 0:1, :] = jnp.sum(jnp.where(diag, west_edge, 0.0), axis=0, keepdims=True)
    top = g == G - 1
    north_slot = jnp.where(top, 1, 0)
    north = pltpu.make_async_remote_copy(
        rim_s.at[0], rim_r.at[north_slot], hsend_sem.at[0], hrecv_sem.at[north_slot],
        device_id=(jnp.where(top, g, g + 1), jnp.where(top, T - 1 - t, t)), device_id_type=MESH)
    south = pltpu.make_async_remote_copy(
        rim_s.at[1], rim_r.at[1], hsend_sem.at[1], hrecv_sem.at[1],
        device_id=(jnp.maximum(g - 1, 0), t), device_id_type=MESH)
    east = pltpu.make_async_remote_copy(
        rim_s.at[2, pl.ds(0, 1)], rim_r.at[2, pl.ds(0, 1)], hsend_sem.at[2], hrecv_sem.at[2],
        device_id=(g, lax.rem(t + 1, T)), device_id_type=MESH)
    west = pltpu.make_async_remote_copy(
        rim_s.at[3, pl.ds(0, 1)], rim_r.at[3, pl.ds(0, 1)], hsend_sem.at[3], hrecv_sem.at[3],
        device_id=(g, lax.rem(t + T - 1, T)), device_id_type=MESH)
    north.start()
    pl.when(g > 0)(south.start)
    east.start()
    west.start()

    sensible = 0.6 * speed * (sea - air_temp)
    latent = 0.7 * speed * (vapor - air_vapor)
    for f, field in enumerate((sea, sensible, latent, long_up)):
        hi, lo = split(field * share)
        for h in range(H):
            surf_v[pl.ds(h, R, stride=H), f, :] = hi[h * R : (h + 1) * R]
            surf_v[pl.ds(h, R, stride=H), NB + f, :] = lo[h * R : (h + 1) * R]

    returns = {}
    zero = jnp.zeros((8, B), f32)
    for d in range(T - 1, -1, -1):
        rows = []
        for c in range(C):
            tile = surf_v[spots[d, c]]
            rows.append(jnp.concatenate([tile if k == c else zero for k in range(C)], axis=1))
        lhs = jnp.concatenate(rows, axis=0).astype(bf16)
        weight = w_v[0, source(d)].reshape(C * B, B)
        prod = jnp.dot(lhs, weight, preferred_element_type=f32)
        tiles = []
        for c in range(C):
            part = prod[c * 8 : (c + 1) * 8]
            tiles.append(part + pltpu.roll(part, NB, 0))
        for c in range(0, C, 2):
            back_v[d, c * NB : (c + 2) * NB, :] = jnp.where(row8 < NB, tiles[c], tiles[c + 1])
        if d:
            returns[d] = pltpu.make_async_remote_copy(
                back_v.at[d], ret_v.at[d], bsend_sem.at[d], brecv_sem.at[d],
                device_id=(g, source(d)), device_id_type=MESH)
            returns[d].start()

    heat_v[...] = jnp.concatenate(
        [((0.94 * short_down + long_down - long_up - sensible - latent) * share)[h * R : (h + 1) * R] for h in range(H)],
        axis=1)
    heat_copy = pltpu.make_async_copy(heat_v, heat, out_sem.at[0])
    heat_copy.start()

    north.wait_send()
    pl.when(g > 0)(south.wait_send)
    south_in = pltpu.make_async_remote_copy(
        rim_s.at[0], rim_r.at[0], hsend_sem.at[0], hrecv_sem.at[0],
        device_id=(jnp.maximum(g - 1, 0), t), device_id_type=MESH)
    pl.when(g > 0)(south_in.wait_recv)
    south.wait_recv()
    east.wait()
    west.wait()
    flip = (iota((B, B), 0) + iota((B, B), 1) == B - 1).astype(f32)
    north_rim = rim_r[1]
    mirrored = jnp.dot(north_rim, flip, precision=lax.Precision.HIGHEST, preferred_element_type=f32)
    row = iota((R, B), 0)
    col = iota((R, B), 1)
    west_col = jnp.sum(jnp.where(diag, rim_r[2, 0:1, :], 0.0), axis=1, keepdims=True)
    east_col = jnp.sum(jnp.where(diag, rim_r[3, 0:1, :], 0.0), axis=1, keepdims=True)
    sx = [stress_x[h * R : (h + 1) * R] for h in range(H)]
    sy = [stress_y[h * R : (h + 1) * R] for h in range(H)]
    ahead = [pltpu.roll(v, B - 1, 1) for v in sy]
    behind = [pltpu.roll(v, 1, 1) for v in sy]
    for h in range(H):
        nxt = ahead[h + 1] if h < H - 1 else east_col
        prv = behind[h - 1] if h else west_col
        dx = jnp.where(col == B - 1, nxt, ahead[h]) - jnp.where(col == 0, prv, behind[h])
        rim_n = jnp.where(top, -mirrored[H - 1 - h : H - h], north_rim[h : h + 1])
        rim_b = jnp.where(g == 0, 0.0, rim_r[0, h : h + 1, :])
        dy = jnp.where(row == R - 1, rim_n, pltpu.roll(sx[h], R - 1, 0)) - jnp.where(
            row == 0, rim_b, pltpu.roll(sx[h], 1, 0))
        curl_v[:, h * B : (h + 1) * B] = (0.5 * dx - 0.5 * dy) * share[h * R : (h + 1) * R]
    curl_copy = pltpu.make_async_copy(curl_v, curl, out_sem.at[1])
    curl_copy.start()

    totals = [zero] * A
    for d in range(T):
        if d:
            returns[d].wait_recv()
        for m in range(C // 2):
            piece = (ret_v if d else back_v)[d, m * 8 : (m + 1) * 8, :]
            home = homes[d * (C // 2) + m]
            for b in range(A):
                totals[b] = totals[b] + jnp.where(home == b, piece, 0.0)
    for b in range(A):
        out_v[:, b * B : (b + 1) * B] = (totals[b] + pltpu.roll(totals[b], NB, 0))[:NB]
    ret_copy = pltpu.make_async_copy(out_v, ret_out, out_sem.at[2])
    ret_copy.start()
    for d in range(1, T):
        outgoing[d].wait_send()
        returns[d].wait_send()
    heat_copy.wait()
    curl_copy.wait()
    ret_copy.wait()


def per_device(mesh, *args):
    atm, sblk, scnt, rblk, wgt, temp, mask = args
    G, T = mesh.shape["grp"], mesh.shape["tile"]
    NF, B, C, NB = atm.shape[0], wgt.shape[-1], sblk.shape[2], 4
    A = atm.shape[1] // B
    R, W = temp.shape
    H = W // B
    dims = (G, T, NF, NB, C, B, A, R, H)
    vm = pltpu.VMEM
    dma = pltpu.SemaphoreType.DMA
    return pl.pallas_call(
        functools.partial(kernel, dims),
        out_shape=(
            jax.ShapeDtypeStruct((R, W), f32),
            jax.ShapeDtypeStruct((R, W), f32),
            jax.ShapeDtypeStruct((NB, A * B), f32),
        ),
        in_specs=[pl.BlockSpec(memory_space=pl.ANY)] * 7,
        out_specs=[pl.BlockSpec(memory_space=pl.ANY)] * 3,
        scratch_shapes=[
            vm((NF, A * B), f32),
            pltpu.SMEM(sblk.shape, jnp.int32),
            pltpu.SMEM(scnt.shape, jnp.int32),
            pltpu.SMEM(rblk.shape, jnp.int32),
            vm(wgt.shape, wgt.dtype),
            vm((R, W), f32),
            vm((R, W), jnp.int32),
            vm((T, NF * C, B), f32),
            vm((T, NF * C, B), f32),
            vm((T * C, NF * B), f32),
            vm((H * R, 8, B), f32),
            vm((T, NB * C, B), f32),
            vm((T, NB * C, B), f32),
            vm((4, H, B), f32),
            vm((4, H, B), f32),
            vm((R, W), f32),
            vm((R, W), f32),
            vm((NB, A * B), f32),
            dma((7,)),
            dma((T,)),
            dma((T,)),
            dma((T,)),
            dma((T,)),
            dma((4,)),
            dma((4,)),
            dma((3,)),
        ],
        compiler_params=pltpu.CompilerParams(collective_id=0, has_side_effects=True),
        name="exchange",
    )(*args)


def solution(mesh):
    placed = (
        P(None, ("grp", "tile")),
        P(("grp", "tile"), None, None),
        P(("grp", "tile"), None),
        P(("grp", "tile"), None, None),
        P(("grp", "tile"), None, None, None, None),
        P("grp", "tile"),
        P("grp", "tile"),
    )
    return jax.shard_map(
        functools.partial(per_device, mesh),
        mesh=mesh,
        in_specs=placed,
        out_specs=(P("grp", "tile"), P("grp", "tile"), P(None, ("grp", "tile"))),
        check_vma=False,
    )
```

time: 38.4 us -> 17.6 us (0.46)
  starting transfers between devices: 20 us -> 0 us
  Pallas kernels: 0 us -> 13.9 us
  waiting for transfers between devices: 5.95 us -> 0 us
  other arithmetic: 3.19 us -> 0 us
  matrix products: 2.61 us -> 0 us
  local copies, waits for them, and re-layouts: 5.32 us -> 2.72 us
    pallas_call x0 -> x1, Pallas kernels: none -> 13.9 us  [per_device(): pl.pallas_call(functools.partial(kernel, dims), out_shape=(jax.ShapeDtype...]
    ppermute x6 -> x0, starting transfers between devices: 10.2 us -> none  [the longest x2 4.99 us: extended(): lax.ppermute(lax.slice_in_dim(block, 0, width, axis=dim), axis, backward)]
    all_to_all x2 -> x0, starting transfers between devices: 9.74 us -> none  [the longest x1 6.48 us: per_device(): lax.all_to_all(chosen, 'tile', split_axis=1, concat_axis=1, tiled=True)]
    all_to_all x2 -> x0, waiting for transfers between devices: 4.65 us -> none  [the longest x1 4.65 us: per_device(): lax.all_to_all(chosen, 'tile', split_axis=1, concat_axis=1, tiled=True)]
    dot_general x4 -> x0, matrix products: 2.61 us -> none  [the longest x1 1.2 us: per_device(): jnp.einsum('scij,fsci->fscj', weight_wide, chosen_back, precision=precise)]
    gather x2 -> x0, local copies, waits for them, and re-layouts: 1.9 us -> none  [the longest x1 1.31 us: per_device(): chosen = jnp.take(blocks, send_index, axis=1) * live_slots[None, :, :, None]]
    mul x4 -> x0, other arithmetic: 1.64 us -> none  [the longest x1 0.72 us: per_device(): stress_curl = stress_curl * sea_share]
    ppermute x6 -> x0, waiting for transfers between devices: 1.3 us -> none  [the longest x2 1.28 us: extended(): lax.ppermute(lax.slice_in_dim(block, block.shape[dim] - width, None, axis...]
  transfers between devices with their start and end apart: 8 -> 0, of which waited for: 2 -> 0; matrix products, arithmetic and copies ran while one was open for 9% -> 0% of each run, Pallas kernels for 0% -> 0%
where the time goes in v1:
time: 17.6 us; the launch traced here: 17.3 us
  Pallas kernels  13.9 us (79%)
  local copies, waits for them, and re-layouts  2.72 us (15%)
  between operations  0.65 us (4%)
    pallas_call x1, Pallas kernels, per_device(): pl.pallas_call(functools.partial(kernel, dims), out_shape=(jax.ShapeDtype...  13.9 us
    unnamed x7, local copies, waits for them, and re-layouts  2.72 us

profile of v1, /device:TPU:0, one launch (start us, length us, event | category | flops | bytes accessed | tf_op | source)
XLA Modules:
  0.0 17.3 jit_solution(1701959094101182479)
XLA Ops:
  0.6 13.9 %exchange.1 = (f32[32,256]{1,0:T(8,128)}, f32[32,256]{1,0:T(8,128)}, f32[4,1024]{1,0:T(4,128)}) custom-call(f32[6,1024]{1,0:T(8,128)} %atm.1, s32[1,4,4]{2,1,0:T(4,128)} %sblk.1, s32[1,4]{1,0:T(1,128)} %scnt.1, s32[1,4,4]{2,1,0:T(4,128)} %rblk.1, bf16[1,4,4,128,128]{4,3,2,1,0:T(8,128)(2,1)} %wgt.1, f32[32,256]{1,0:T(8,128)} %temp.1, s32[32,256]{1,0:T(8,128)} %mask.1), custom_call_target="tpu_custom_call" | custom-call | tf_op jit(solution)/shard_map/exchange/pallas_call | solution.py:258
  14.6 0.0 copy-start
  14.6 1.4 %copy.13 = f32[32,256]{1,0:T(8,128)} copy(f32[32,256]{1,0:T(8,128)} %get-tuple-element.6) | data formatting | bytes 65536
  16.0 0.0 copy-done
  16.0 0.0 copy-start.1
  16.0 0.6 %copy.14 = f32[32,256]{1,0:T(8,128)} copy(f32[32,256]{1,0:T(8,128)S(1)} %copy-done) | data formatting | bytes 65536
  16.6 0.1 copy-done.1
  16.7 0.6 %copy.15 = f32[4,1024]{1,0:T(4,128)} copy(f32[4,1024]{1,0:T(4,128)S(1)} %copy-done.1) | data formatting | bytes 32768
Async XLA Ops:
  14.6 1.4 %copy-start = (f32[32,256]{1,0:T(8,128)S(1)}, f32[32,256]{1,0:T(8,128)}, u32[]{:S(2)}) copy-start(f32[32,256]{1,0:T(8,128)} %get-tuple-element.7) | copy-start | bytes 98308
  16.0 0.7 %copy-start.1 = (f32[4,1024]{1,0:T(4,128)S(1)}, f32[4,1024]{1,0:T(4,128)}, u32[]{:S(2)}) copy-start(f32[4,1024]{1,0:T(4,128)} %get-tuple-element.8) | copy-start | bytes 49156

commit v2 on v1

--- a/solution.py
+++ b/solution.py
@@ -20,10 +20,10 @@
     return lax.broadcasted_iota(jnp.int32, shape, dim)
 
 
-def kernel(dims, atm, sblk, scnt, rblk, wgt, temp, mask, heat, curl, ret_out,
+def kernel(dims, atm, sblk, scnt, rblk, wgt, temp, mask, heat_v, curl_v, out_v,
            atm_v, sblk_s, scnt_s, rblk_s, w_v, temp_v, mask_v, send_v, recv_v, rhs_v, surf_v,
-           back_v, ret_v, rim_s, rim_r, heat_v, curl_v, out_v,
-           in_sem, send_sem, recv_sem, bsend_sem, brecv_sem, hsend_sem, hrecv_sem, out_sem):
+           back_v, ret_v, rim_s, rim_r,
+           in_sem, send_sem, recv_sem, bsend_sem, brecv_sem, hsend_sem, hrecv_sem):
     G, T, NF, NB, C, B, A, R, H = dims
     nk = T * C
     g = lax.axis_index("grp")
@@ -189,8 +189,6 @@
     heat_v[...] = jnp.concatenate(
         [((0.94 * short_down + long_down - long_up - sensible - latent) * share)[h * R : (h + 1) * R] for h in range(H)],
         axis=1)
-    heat_copy = pltpu.make_async_copy(heat_v, heat, out_sem.at[0])
-    heat_copy.start()
 
     north.wait_send()
     pl.when(g > 0)(south.wait_send)
@@ -221,8 +219,6 @@
         dy = jnp.where(row == R - 1, rim_n, pltpu.roll(sx[h], R - 1, 0)) - jnp.where(
             row == 0, rim_b, pltpu.roll(sx[h], 1, 0))
         curl_v[:, h * B : (h + 1) * B] = (0.5 * dx - 0.5 * dy) * share[h * R : (h + 1) * R]
-    curl_copy = pltpu.make_async_copy(curl_v, curl, out_sem.at[1])
-    curl_copy.start()
 
     totals = [zero] * A
     for d in range(T):
@@ -235,14 +231,17 @@
                 totals[b] = totals[b] + jnp.where(home == b, piece, 0.0)
     for b in range(A):
         out_v[:, b * B : (b + 1) * B] = (totals[b] + pltpu.roll(totals[b], NB, 0))[:NB]
-    ret_copy = pltpu.make_async_copy(out_v, ret_out, out_sem.at[2])
-    ret_copy.start()
     for d in range(1, T):
         outgoing[d].wait_send()
         returns[d].wait_send()
-    heat_copy.wait()
-    curl_copy.wait()
-    ret_copy.wait()
+
+
+def put_out(a, b, c, x, y, z, sem):
+    copies = [pltpu.make_async_copy(src, dst, sem.at[k]) for k, (src, dst) in enumerate(((a, x), (b, y), (c, z)))]
+    for copy in copies:
+        copy.start()
+    for copy in copies:
+        copy.wait()
 
 
 def per_device(mesh, *args):
@@ -255,15 +254,11 @@
     dims = (G, T, NF, NB, C, B, A, R, H)
     vm = pltpu.VMEM
     dma = pltpu.SemaphoreType.DMA
-    return pl.pallas_call(
+    held = pl.pallas_call(
         functools.partial(kernel, dims),
-        out_shape=(
-            jax.ShapeDtypeStruct((R, W), f32),
-            jax.ShapeDtypeStruct((R, W), f32),
-            jax.ShapeDtypeStruct((NB, A * B), f32),
-        ),
+        out_shape=(vm((R, W), f32), vm((R, W), f32), vm((NB, A * B), f32)),
         in_specs=[pl.BlockSpec(memory_space=pl.ANY)] * 7,
-        out_specs=[pl.BlockSpec(memory_space=pl.ANY)] * 3,
+        out_specs=[pl.BlockSpec(memory_space=vm)] * 3,
         scratch_shapes=[
             vm((NF, A * B), f32),
             pltpu.SMEM(sblk.shape, jnp.int32),
@@ -280,9 +275,6 @@
             vm((T, NB * C, B), f32),
             vm((4, H, B), f32),
             vm((4, H, B), f32),
-            vm((R, W), f32),
-            vm((R, W), f32),
-            vm((NB, A * B), f32),
             dma((7,)),
             dma((T,)),
             dma((T,)),
@@ -290,11 +282,18 @@
             dma((T,)),
             dma((4,)),
             dma((4,)),
-            dma((3,)),
         ],
         compiler_params=pltpu.CompilerParams(collective_id=0, has_side_effects=True),
         name="exchange",
     )(*args)
+    return pl.pallas_call(
+        put_out,
+        out_shape=[jax.ShapeDtypeStruct(v.shape, v.dtype) for v in held],
+        in_specs=[pl.BlockSpec(memory_space=vm)] * 3,
+        out_specs=[pl.BlockSpec(memory_space=pl.ANY)] * 3,
+        scratch_shapes=[dma((3,))],
+        name="put_out",
+    )(*[pltpu.with_memory_space_constraint(v, vm) for v in held])
 
 
 def solution(mesh):

time: 17.6 us -> 14.8 us (0.84)
  local copies, waits for them, and re-layouts: 2.72 us -> 0 us
    unnamed x7 -> x0, local copies, waits for them, and re-layouts: 2.72 us -> none
    pallas_call x1 -> x2, Pallas kernels: 13.9 us -> 14 us  [the longest x1 13.3 us: per_device(): pl.pallas_call(functools.partial(kernel, dims), out_shape=(vm((R, W), f32...]
where the time goes in v2:
time: 14.8 us; the launch traced here: 14.6 us
  Pallas kernels  14 us (95%)
  between operations  0.64 us (4%)
    pallas_call x1, Pallas kernels, per_device(): pl.pallas_call(functools.partial(kernel, dims), out_shape=(vm((R, W), f32...  13.3 us
    pallas_call x1, Pallas kernels, per_device(): pl.pallas_call(put_out, out_shape=[jax.ShapeDtypeStruct(v.shape, v.dtype)...  0.66 us

profile of v2, /device:TPU:0, one launch (start us, length us, event | category | flops | bytes accessed | tf_op | source)
XLA Modules:
  0.0 14.6 jit_solution(16943867969708951569)
XLA Ops:
  0.6 13.3 %exchange.1 = (f32[32,256]{1,0:T(8,128)S(1)}, f32[32,256]{1,0:T(8,128)S(1)}, f32[4,1024]{1,0:T(4,128)S(1)}) custom-call(f32[6,1024]{1,0:T(8,128)} %atm.1, s32[1,4,4]{2,1,0:T(4,128)} %sblk.1, s32[1,4]{1,0:T(1,128)} %scnt.1, s32[1,4,4]{2,1,0:T(4,128)} %rblk.1, bf16[1,4,4,128,128]{4,3,2,1,0:T(8,128)(2,1)} %wgt.1, f32[32,256]{1,0:T(8,128)} %temp.1, s32[32,256]{1,0:T(8,128)} %mask.1), custom_call_target="tpu_custom_call" | custom-call | tf_op jit(solution)/shard_map/exchange/pallas_call | solution.py:257
  14.0 0.7 %put_out.1 = (f32[32,256]{1,0:T(8,128)}, f32[32,256]{1,0:T(8,128)}, f32[4,1024]{1,0:T(4,128)}) custom-call(f32[32,256]{1,0:T(8,128)S(1)} %get-tuple-element.6.a, f32[32,256]{1,0:T(8,128)S(1)} %get-tuple-element.7.b, f32[4,1024]{1,0:T(4,128)S(1)} %get-tuple-element.8.c), custom_call_target="tpu_custom_call" | custom-call | tf_op jit(solution)/shard_map/put_out/pallas_call | solution.py:289

commit v3 on v2

--- a/solution.py
+++ b/solution.py
@@ -21,8 +21,7 @@
 
 
 def kernel(dims, atm, sblk, scnt, rblk, wgt, temp, mask, heat_v, curl_v, out_v,
-           atm_v, sblk_s, scnt_s, rblk_s, w_v, temp_v, mask_v, send_v, recv_v, rhs_v, surf_v,
-           back_v, ret_v, rim_s, rim_r,
+           atm_v, sblk_s, scnt_s, rblk_s, w_v, temp_v, mask_v, send_v, recv_v, back_v, ret_v, rim_s, rim_r,
            in_sem, send_sem, recv_sem, bsend_sem, brecv_sem, hsend_sem, hrecv_sem):
     G, T, NF, NB, C, B, A, R, H = dims
     nk = T * C
@@ -74,7 +73,7 @@
     outgoing = {}
     for d in range(T - 1, 0, -1):
         outgoing[d] = pltpu.make_async_remote_copy(
-            send_v.at[d], recv_v.at[d], send_sem.at[d], recv_sem.at[d],
+            send_v.at[d], recv_v.at[d], send_sem.at[0], recv_sem.at[d - 1],
             device_id=(g, target(d)), device_id_type=MESH)
         outgoing[d].start()
 
@@ -87,26 +86,34 @@
     base = 1.0 + 0.2 * sea
     base = base * base
     long_up = 0.4 * (base * base)
-    lane = iota((8, 2 * nk), 1)
-    place = jnp.full((8, 2 * nk), -1, jnp.int32)
-    spots = {}
+    per = 2 * C
+    cells = H * R
+    order = lambda o: (o % R) * H + o // R
+    lane = iota((8, 2 * T * per), 1)
+    row8 = iota((8, B), 0)
+    place = jnp.full((8, 2 * T * per), -1, jnp.int32)
+    picks, homes = [], []
+    col = iota((per, 2 * cells), 1)
+    prow = iota((per, 2 * cells), 0)
     for d in range(T):
+        pick = jnp.full((per, 2 * cells), -1, jnp.int32)
+        home = jnp.full((8, B), -1, jnp.int32)
         for c in range(C):
             o = rblk_s[0, source(d), c]
-            spots[d, c] = o
-            k = d * C + c
-            place = jnp.where((lane == k) | (lane == nk + k), o, place)
-    where_row = iota((H * R, 2 * nk), 0)
-    where_row = (where_row % R) * H + where_row // R
-    onehot = (where_row == place[0:1]).astype(f32).astype(bf16)
-    row8 = iota((8, B), 0)
-    homes = []
-    for d in range(T):
-        for c in range(0, C, 2):
-            homes.append(jnp.where(row8 < NB, wanted[d, c], wanted[d, c + 1]))
+            place = jnp.where((lane // per % T == d) & (lane % C == c), o, place)
+            pick = jnp.where(prow % C == c, o, pick)
+            home = jnp.where(row8 % C == c, wanted[d, c], home)
+        picks.append(jnp.where((order(col % cells) == pick) & (col // cells == prow // C), 1.0, 0.0))
+        homes.append(home)
+    gather = jnp.concatenate(picks, axis=0).astype(bf16)
+    land_row = iota((2 * cells, 2 * T * per), 0)
+    land_col = iota((2 * cells, 2 * T * per), 1)
+    onehot = jnp.where(
+        (order(land_row % cells) == place[0:1]) & (land_row // cells == land_col % per // C), 1.0, 0.0).astype(bf16)
     loads[6].wait()
 
     rowf = iota((NF * C, B), 0) % C
+    parts = []
     for d in range(T):
         if d:
             outgoing[d].wait_recv()
@@ -119,12 +126,12 @@
         mine = prod[:, :B]
         for c in range(1, C):
             mine = jnp.where(rowf == c, prod[:, c * B : (c + 1) * B], mine)
-        for f in range(NF):
-            rhs_v[d * C : (d + 1) * C, f * B : (f + 1) * B] = mine[f * C : (f + 1) * C]
-
-    hi, lo = split(rhs_v[...])
+        parts.append(jnp.concatenate([mine[k * per : (k + 1) * per] for k in range(NF // 2)], axis=1))
+
+    hi, lo = split(jnp.concatenate(parts, axis=0))
     landed = jnp.dot(onehot, jnp.concatenate([hi, lo], axis=0).astype(bf16), preferred_element_type=f32)
-    wind_u, wind_v, air_temp, air_vapor, short_down, long_down = [landed[:, f * B : (f + 1) * B] for f in range(NF)]
+    wind_u, wind_v, air_temp, air_vapor, short_down, long_down = [
+        landed[f % 2 * cells : (f % 2 + 1) * cells, f // 2 * B : (f // 2 + 1) * B] for f in range(NF)]
     speed = jnp.sqrt(wind_u * wind_u + wind_v * wind_v + 0.5)
     stress_x = 0.8 * speed * wind_u * share
     stress_y = 0.8 * speed * wind_v * share
@@ -158,31 +165,25 @@
 
     sensible = 0.6 * speed * (sea - air_temp)
     latent = 0.7 * speed * (vapor - air_vapor)
-    for f, field in enumerate((sea, sensible, latent, long_up)):
-        hi, lo = split(field * share)
-        for h in range(H):
-            surf_v[pl.ds(h, R, stride=H), f, :] = hi[h * R : (h + 1) * R]
-            surf_v[pl.ds(h, R, stride=H), NB + f, :] = lo[h * R : (h + 1) * R]
+    pieces = [split(field * share) for field in (sea, sensible, latent, long_up)]
+    surface = jnp.concatenate(
+        [jnp.concatenate([pieces[2 * k + e][p] for p in range(2) for k in range(NB // 2)], axis=1) for e in range(2)],
+        axis=0).astype(bf16)
+    chosen = jnp.dot(gather, surface, preferred_element_type=f32)
 
     returns = {}
     zero = jnp.zeros((8, B), f32)
+    rowb = iota((2 * NB * C, B), 0) % C
     for d in range(T - 1, -1, -1):
-        rows = []
-        for c in range(C):
-            tile = surf_v[spots[d, c]]
-            rows.append(jnp.concatenate([tile if k == c else zero for k in range(C)], axis=1))
-        lhs = jnp.concatenate(rows, axis=0).astype(bf16)
+        tile = chosen[d * per : (d + 1) * per]
+        tile = jnp.concatenate([tile[:, k * B : (k + 1) * B] for k in range(NB)], axis=0)
+        lhs = jnp.concatenate([jnp.where(rowb == c, tile, 0.0) for c in range(C)], axis=1).astype(bf16)
         weight = w_v[0, source(d)].reshape(C * B, B)
         prod = jnp.dot(lhs, weight, preferred_element_type=f32)
-        tiles = []
-        for c in range(C):
-            part = prod[c * 8 : (c + 1) * 8]
-            tiles.append(part + pltpu.roll(part, NB, 0))
-        for c in range(0, C, 2):
-            back_v[d, c * NB : (c + 2) * NB, :] = jnp.where(row8 < NB, tiles[c], tiles[c + 1])
+        back_v[d] = prod[: NB * C] + prod[NB * C :]
         if d:
             returns[d] = pltpu.make_async_remote_copy(
-                back_v.at[d], ret_v.at[d], bsend_sem.at[d], brecv_sem.at[d],
+                back_v.at[d], ret_v.at[d], bsend_sem.at[0], brecv_sem.at[0],
                 device_id=(g, source(d)), device_id_type=MESH)
             returns[d].start()
 
@@ -220,20 +221,22 @@
             row == 0, rim_b, pltpu.roll(sx[h], 1, 0))
         curl_v[:, h * B : (h + 1) * B] = (0.5 * dx - 0.5 * dy) * share[h * R : (h + 1) * R]
 
-    totals = [zero] * A
+    others = pl.ds(1, T - 1)
+    whole = lambda ref, sem: pltpu.make_async_copy(ref.at[others], ref.at[others], sem.at[0])
+    totals = {(b, k): zero for b in range(A) for k in range(NB // 2)}
     for d in range(T):
-        if d:
-            returns[d].wait_recv()
-        for m in range(C // 2):
-            piece = (ret_v if d else back_v)[d, m * 8 : (m + 1) * 8, :]
-            home = homes[d * (C // 2) + m]
+        if d == 1:
+            whole(ret_v, brecv_sem).wait()
+        for k in range(NB // 2):
+            piece = (ret_v if d else back_v)[d, k * per : (k + 1) * per, :]
             for b in range(A):
-                totals[b] = totals[b] + jnp.where(home == b, piece, 0.0)
+                totals[b, k] = totals[b, k] + jnp.where(homes[d] == b, piece, 0.0)
     for b in range(A):
-        out_v[:, b * B : (b + 1) * B] = (totals[b] + pltpu.roll(totals[b], NB, 0))[:NB]
-    for d in range(1, T):
-        outgoing[d].wait_send()
-        returns[d].wait_send()
+        for k in range(NB // 2):
+            v = totals[b, k].reshape(2, C, B).sum(axis=1)
+            out_v[2 * k : 2 * k + 2, b * B : (b + 1) * B] = v
+    whole(send_v, send_sem).wait()
+    whole(back_v, bsend_sem).wait()
 
 
 def put_out(a, b, c, x, y, z, sem):
@@ -269,17 +272,15 @@
             vm((R, W), jnp.int32),
             vm((T, NF * C, B), f32),
             vm((T, NF * C, B), f32),
-            vm((T * C, NF * B), f32),
-            vm((H * R, 8, B), f32),
             vm((T, NB * C, B), f32),
             vm((T, NB * C, B), f32),
             vm((4, H, B), f32),
             vm((4, H, B), f32),
             dma((7,)),
-            dma((T,)),
-            dma((T,)),
-            dma((T,)),
-            dma((T,)),
+            dma((1,)),
+            dma((T - 1,)),
+            dma((1,)),
+            dma((1,)),
             dma((4,)),
             dma((4,)),
         ],

time: 14.8 us -> 14.6 us (0.986)
  Pallas kernels: 14 us -> 13.8 us
    pallas_call x1, Pallas kernels: 13.3 us -> 13.1 us  [per_device(): pl.pallas_call(functools.partial(kernel, dims), out_shape=(vm((R, W), f32...]
where the time goes in v3:
time: 14.6 us; the launch traced here: 14.4 us
  Pallas kernels  13.8 us (95%)
  between operations  0.64 us (4%)
    pallas_call x1, Pallas kernels, per_device(): pl.pallas_call(functools.partial(kernel, dims), out_shape=(vm((R, W), f32...  13.1 us
    pallas_call x1, Pallas kernels, per_device(): pl.pallas_call(put_out, out_shape=[jax.ShapeDtypeStruct(v.shape, v.dtype)...  0.66 us

profile of v3, /device:TPU:0, one launch (start us, length us, event | category | flops | bytes accessed | tf_op | source)
XLA Modules:
  0.0 14.4 jit_solution(5828649655844861822)
XLA Ops:
  0.6 13.1 %exchange.1 = (f32[32,256]{1,0:T(8,128)S(1)}, f32[32,256]{1,0:T(8,128)S(1)}, f32[4,1024]{1,0:T(4,128)S(1)}) custom-call(f32[6,1024]{1,0:T(8,128)} %atm.1, s32[1,4,4]{2,1,0:T(4,128)} %sblk.1, s32[1,4]{1,0:T(1,128)} %scnt.1, s32[1,4,4]{2,1,0:T(4,128)} %rblk.1, bf16[1,4,4,128,128]{4,3,2,1,0:T(8,128)(2,1)} %wgt.1, f32[32,256]{1,0:T(8,128)} %temp.1, s32[32,256]{1,0:T(8,128)} %mask.1), custom_call_target="tpu_custom_call" | custom-call | tf_op jit(solution)/shard_map/exchange/pallas_call | solution.py:260
  13.7 0.7 %put_out.1 = (f32[32,256]{1,0:T(8,128)}, f32[32,256]{1,0:T(8,128)}, f32[4,1024]{1,0:T(4,128)}) custom-call(f32[32,256]{1,0:T(8,128)S(1)} %get-tuple-element.6.a, f32[32,256]{1,0:T(8,128)S(1)} %get-tuple-element.7.b, f32[4,1024]{1,0:T(4,128)S(1)} %get-tuple-element.8.c), custom_call_target="tpu_custom_call" | custom-call | tf_op jit(solution)/shard_map/put_out/pallas_call | solution.py:290
